TPU v7x, 32 devices: a whole 2x2x4 slice. The times are simulated.
32 devices in a mesh: ep: 4 (over y, x), fsdp: 8 (over z, core).
Axes of the slice: x: 2, y: 2, z: 4, core: 2. Of those that a mesh axis runs over, the one named last changes fastest.
Arguments:
- train_gate: float32 [64, 2048, 1408], P('ep', 'fsdp'), may hold values from -0.1875 to 0.1875
- train_up: float32 [64, 2048, 1408], P('ep', 'fsdp'), may hold values from -0.1875 to 0.1875
- train_down: float32 [64, 1408, 2048], P('ep', None, 'fsdp'), may hold values from -0.21875 to 0.21875
- router_weight: float32 [2048, 64], P('fsdp', 'ep'), may hold values from -0.125 to 0.125
- router_gain: float32 [2048], P('fsdp'), may hold values from 0.25 to 1.75
Outputs:
- ready_gate: bfloat16 [64, 2048, 1408], P('ep', None, 'fsdp')
- ready_up: bfloat16 [64, 2048, 1408], P('ep', None, 'fsdp')
- ready_down: bfloat16 [64, 1408, 2048], P('ep', 'fsdp')
- scale_gate: float32 [64, 1408], P('ep', 'fsdp')
- scale_up: float32 [64, 1408], P('ep', 'fsdp')
- scale_down: float32 [64, 1408], P('ep', 'fsdp')
- serve_router: bfloat16 [2048, 64], replicated
All inputs are finite; a program needn't handle non-finite values. Where the computation divides by a largest or mean magnitude, that divisor is 1e-20 or more.
Results may differ from a plain program's by a relative error of at most 0.001.
Values may be sent and summed in bfloat16 or wider, within the bound.
A program may use at most 256 MiB of HBM per device.

v0:
```python
import jax
import jax.numpy as jnp
from jax import lax
from jax.sharding import PartitionSpec as P


def per_device(train_gate, train_up, train_down, router_weight, router_gain):
    scale_gate, scale_up, scale_down = lax.pmax(
        (
            jnp.max(jnp.abs(train_gate), axis=1),
            jnp.max(jnp.abs(train_up), axis=1),
            jnp.max(jnp.abs(train_down), axis=2),
        ),
        "fsdp",
    )
    narrow_gate, narrow_up, narrow_down = (
        (train_gate / jnp.expand_dims(scale_gate, 1)).astype(jnp.bfloat16),
        (train_up / jnp.expand_dims(scale_up, 1)).astype(jnp.bfloat16),
        (train_down / jnp.expand_dims(scale_down, 2)).astype(jnp.bfloat16),
    )
    ready_gate, ready_up = (
        lax.all_to_all(narrow_gate, "fsdp", split_axis=2, concat_axis=1, tiled=True),
        lax.all_to_all(narrow_up, "fsdp", split_axis=2, concat_axis=1, tiled=True),
    )
    ready_down = lax.all_to_all(narrow_down, "fsdp", split_axis=1, concat_axis=2, tiled=True)
    scale_gate = lax.dynamic_slice_in_dim(
        scale_gate, lax.axis_index("fsdp") * ready_gate.shape[2], ready_gate.shape[2], axis=1
    )
    scale_up = lax.dynamic_slice_in_dim(
        scale_up, lax.axis_index("fsdp") * ready_up.shape[2], ready_up.shape[2], axis=1
    )
    scale_down = lax.dynamic_slice_in_dim(
        scale_down, lax.axis_index("fsdp") * ready_down.shape[1], ready_down.shape[1], axis=1
    )
    part_router = (router_weight * router_gain[:, None]).astype(jnp.bfloat16)
    row_router = lax.all_gather(part_router, "fsdp", axis=0, tiled=True)
    serve_router = lax.all_gather(row_router, "ep", axis=1, tiled=True)
    return (ready_gate, ready_up, ready_down, scale_gate, scale_up, scale_down, serve_router)


def solution(mesh):
    placed = (
        P("ep", "fsdp", None),
        P("ep", "fsdp", None),
        P("ep", None, "fsdp"),
        P("fsdp", "ep"),
        P("fsdp"),
    )
    return jax.shard_map(
        per_device,
        mesh=mesh,
        in_specs=placed,
        out_specs=(
            P("ep", None, "fsdp"),
            P("ep", None, "fsdp"),
            P("ep", "fsdp", None),
            P("ep", "fsdp"),
            P("ep", "fsdp"),
            P("ep", "fsdp"),
            P(),
        ),
        check_vma=False,
    )
```

profile of v0, /device:TPU:0, one launch (start us, length us, event | category | flops | bytes accessed | tf_op | source)
XLA Modules:
  0.0 985.2 jit_solution(7565016768209817902)
XLA Ops:
  7.2 0.0 all-reduce.3.cloned.1.call-start
  7.2 0.0 slice-start
  7.2 10.5 %abs_reduce_fusion = f32[16,1408]{1,0:T(8,128)} fusion(f32[16,1408,256]{2,1,0:T(8,128)} %param.7), kind=kLoop, calls=%fused_computation.2 | loop fusion | flops 11511808 | bytes 23158784 | tf_op jit(solution)/shard_map/reduce_max | solution.py:12
  17.7 10.8 %abs_reduce_fusion.1 = f32[16,1408]{1,0:T(8,128)} fusion(f32[16,256,1408]{2,1,0:T(8,128)} %param.6), kind=kLoop, calls=%fused_computation.4 | loop fusion | flops 11511808 | bytes 23158784 | tf_op jit(solution)/shard_map/reduce_max | solution.py:11
  28.6 2.4 abs_reduce_fusion.2
  31.0 0.0 all-reduce.3.cloned.1.call-update
  31.0 23.7 %copy.24 = f32[16,256,1408]{1,0,2:T(8,128)} copy(f32[16,256,1408]{2,1,0:T(8,128)} %param.5) | data formatting | bytes 46137344 | tf_op args[0]
  54.7 32.5 %all-reduce.3.cloned.1.call-done = (f32[16,1408]{1,0:T(8,128)}, f32[16,1408]{1,0:T(8,128)}, f32[16,1408]{1,0:T(8,128)}) async-done(((f32[16,1408]{1,0:T(8,128)}, f32[16,1408]{1,0:T(8,128)}, f32[16,1408]{1,0:T(8,128)}), (f32[16,1408]{1,0:T(8,128)}, f32[16,1408]{1,0:T(8,128)}, f32[16,1408]{1,0:T(8,128)})) %all-reduce.3.cloned.1.call-update) | async-done | bytes 270352 | tf_op jit(solution)/shard_map/pmax | solution.py:8
  87.2 1.1 copy.23
  88.4 14.2 %divide_convert_fusion.1 = bf16[16,256,1408]{1,0,2:T(8,128)(2,1)} fusion(f32[16,256,1408]{1,0,2:T(8,128)} %copy.24, f32[16,1408]{0,1:T(8,128)S(1)} %copy.23), kind=kLoop, calls=%fused_computation.5 | loop fusion | flops 11534336 | bytes 34693120 | tf_op jit(solution)/shard_map/convert_element_type | solution.py:17
  102.6 5.4 all-to-all-start
  108.0 23.7 %copy.28 = f32[16,256,1408]{1,0,2:T(8,128)} copy(f32[16,256,1408]{2,1,0:T(8,128)} %param.6) | data formatting | bytes 46137344 | tf_op args[1]
  131.7 0.3 copy.27
  132.0 14.2 %divide_convert_fusion = bf16[16,256,1408]{1,0,2:T(8,128)(2,1)} fusion(f32[16,256,1408]{1,0,2:T(8,128)} %copy.28, f32[16,1408]{0,1:T(8,128)S(1)} %copy.27), kind=kLoop, calls=%fused_computation.3 | loop fusion | flops 11534336 | bytes 34693120 | tf_op jit(solution)/shard_map/convert_element_type | solution.py:18
  146.2 213.1 %all-to-all-done = bf16[16,256,1408]{1,0,2:T(8,128)(2,1)} async-done(((bf16[16,256,1408]{1,0,2:T(8,128)(2,1)}), bf16[16,256,1408]{1,0,2:T(8,128)(2,1)}, u32[]{:S(2)}, u32[]{:S(2)}) %all-to-all-start) | async-done | bytes 11534368 | tf_op jit(solution)/shard_map/all_to_all | solution.py:22
  359.4 5.2 all-to-all-start.1
  364.6 0.3 copy.31
  364.9 0.0 copy-start.3
  364.9 32.6 %fusion = bf16[16,1408,256]{2,0,1:T(8,128)(2,1)} fusion(f32[16,1408,256]{2,1,0:T(8,128)} %param.7, f32[16,1408]{0,1:T(8,128)S(1)} %copy.31), kind=kLoop, calls=%fused_computation.1 | loop fusion | flops 11534336 | bytes 34693120 | tf_op jit(solution)/shard_map/convert_element_type | solution.py:19
  397.5 218.4 %all-to-all-done.1 = bf16[16,256,1408]{1,0,2:T(8,128)(2,1)} async-done(((bf16[16,256,1408]{1,0,2:T(8,128)(2,1)}), bf16[16,256,1408]{1,0,2:T(8,128)(2,1)}, u32[]{:S(2)}, u32[]{:S(2)}) %all-to-all-start.1) | async-done | bytes 11534368 | tf_op jit(solution)/shard_map/all_to_all | solution.py:23
  615.9 5.3 all-to-all-start.2
  621.3 257.3 %all_gather.6 = bf16[2048,16]{0,1:T(8,128)(2,1)S(1)} all-gather(bf16[256,16]{0,1:T(8,128)(2,1)S(1)} %multiply_convert_fusion), channel_id=1, replica_groups=mesh['ep'=4,'fsdp'=8] {'fsdp'}, dimensions={0}, use_global_device_ids=true | all-gather | bytes 73728 | tf_op jit(solution)/shard_map/all_gather | solution.py:36
  878.5 9.1 all_gather.7
  887.7 1.4 constant_dynamic-slice_fusion.2
  889.1 0.7 constant_dynamic-slice_fusion
  889.8 11.3 %copy.26 = bf16[16,8,256,176]{2,1,3,0:T(8,128)(2,1)} copy(bf16[16,8,256,176]{2,0,3,1:T(8,128)(2,1)} %bitcast.2) | data formatting | bytes 23068672 | tf_op jit(solution)/shard_map/all_to_all | solution.py:22
  901.1 18.0 %all_to_all.42 = bf16[16,2048,176]{1,2,0:T(8,128)(2,1)} reshape(bf16[16,8,256,176]{2,1,3,0:T(8,128)(2,1)} %copy.26) | data formatting | bytes 23068672 | tf_op jit(solution)/shard_map/all_to_all | solution.py:22
  919.1 11.3 %copy.30 = bf16[16,8,256,176]{2,1,3,0:T(8,128)(2,1)} copy(bf16[16,8,256,176]{2,0,3,1:T(8,128)(2,1)} %bitcast.5) | data formatting | bytes 23068672 | tf_op jit(solution)/shard_map/all_to_all | solution.py:23
  930.4 18.0 %all_to_all.46 = bf16[16,2048,176]{1,2,0:T(8,128)(2,1)} reshape(bf16[16,8,256,176]{2,1,3,0:T(8,128)(2,1)} %copy.30) | data formatting | bytes 23068672 | tf_op jit(solution)/shard_map/all_to_all | solution.py:23
  948.4 11.4 %copy.33 = bf16[16,176,8,256]{3,2,1,0:T(8,128)(2,1)} copy(bf16[16,176,8,256]{3,0,1,2:T(8,128)(2,1)} %bitcast.7) | data formatting | bytes 23068672 | tf_op jit(solution)/shard_map/all_to_all | solution.py:25
  959.7 18.0 %all_to_all.50 = bf16[16,176,2048]{2,1,0:T(8,128)(2,1)} reshape(bf16[16,176,8,256]{3,2,1,0:T(8,128)(2,1)} %copy.33) | data formatting | bytes 23068672 | tf_op jit(solution)/shard_map/all_to_all | solution.py:25
  977.7 0.7 copy.43
  (21 shorter events, 0.0 us)
Async XLA Ops:
  7.2 80.1 %all-reduce.3.cloned.1.call-start = ((), (), s32[]{:S(2)}) async-start(), calls=%async_computation.3 | async-start | bytes 540672 | tf_op jit(solution)/shard_map/pmax | solution.py:8
  7.2 21.3 %slice-start = ((s8[23068672]{0:T(1024)(128)(4,1)}), s8[4194304]{0:T(1024)(128)(4,1)S(1)}, s32[]{:S(2)}) async-start(s8[23068672]{0:T(1024)(128)(4,1)} %bitcast.19), calls=%async_computation.4 | async-start | bytes 8388608
  7.2 21.3 %slice-start.1 = ((s8[23068672]{0:T(1024)(128)(4,1)}), s8[4194304]{0:T(1024)(128)(4,1)S(1)}, s32[]{:S(2)}) async-start(s8[23068672]{0:T(1024)(128)(4,1)} %bitcast.19), calls=%async_computation.5 | async-start | bytes 8388608
  7.2 21.3 %slice-start.2 = ((s8[23068672]{0:T(1024)(128)(4,1)}), s8[4194304]{0:T(1024)(128)(4,1)S(1)}, s32[]{:S(2)}) async-start(s8[23068672]{0:T(1024)(128)(4,1)} %bitcast.19), calls=%async_computation.6 | async-start | bytes 8388608
  17.7 10.8 %slice-start.3 = ((s8[23068672]{0:T(1024)(128)(4,1)}), s8[4194304]{0:T(1024)(128)(4,1)S(1)}, s32[]{:S(2)}) async-start(s8[23068672]{0:T(1024)(128)(4,1)} %bitcast.19), calls=%async_computation.7 | async-start | bytes 8388608
  17.7 10.8 %slice-start.4 = ((s8[23068672]{0:T(1024)(128)(4,1)}), s8[4194304]{0:T(1024)(128)(4,1)S(1)}, s32[]{:S(2)}) async-start(s8[23068672]{0:T(1024)(128)(4,1)} %bitcast.19), calls=%async_computation.8 | async-start | bytes 8388608
  17.7 10.9 %slice-start.5 = ((s8[23068672]{0:T(1024)(128)(4,1)}), s8[2097152]{0:T(1024)(128)(4,1)S(1)}, s32[]{:S(2)}) async-start(s8[23068672]{0:T(1024)(128)(4,1)} %bitcast.19), calls=%async_computation.9 | async-start | bytes 4194304
  102.6 256.8 %all-to-all-start = ((bf16[16,256,1408]{1,0,2:T(8,128)(2,1)}), bf16[16,256,1408]{1,0,2:T(8,128)(2,1)}, u32[]{:S(2)}, u32[]{:S(2)}) async-start(bf16[16,256,1408]{1,0,2:T(8,128)(2,1)} %divide_convert_fusion.1), calls=%async_computation | async-start | bytes 23068672 | tf_op jit(solution)/shard_map/all_to_all | solution.py:22
  108.0 23.7 %copy-start = (f32[16,1408]{1,0:T(8,128)S(1)}, f32[16,1408]{1,0:T(8,128)}, u32[]{:S(2)}) copy-start(f32[16,1408]{1,0:T(8,128)} %get-tuple-element.8) | copy-start | bytes 270340
  132.0 232.6 %copy-start.1 = (f32[16,1408]{1,0:T(8,128)S(1)}, f32[16,1408]{1,0:T(8,128)}, u32[]{:S(2)}) copy-start(f32[16,1408]{1,0:T(8,128)} %get-tuple-element.9) | copy-start | bytes 270340
  359.4 256.5 %all-to-all-start.1 = ((bf16[16,256,1408]{1,0,2:T(8,128)(2,1)}), bf16[16,256,1408]{1,0,2:T(8,128)(2,1)}, u32[]{:S(2)}, u32[]{:S(2)}) async-start(bf16[16,256,1408]{1,0,2:T(8,128)(2,1)} %divide_convert_fusion), calls=%async_computation.1 | async-start | bytes 23068672 | tf_op jit(solution)/shard_map/all_to_all | solution.py:23
  364.9 256.3 %copy-start.2 = (f32[256,16]{0,1:T(8,128)S(1)}, f32[256,16]{0,1:T(8,128)}, u32[]{:S(2)}) copy-start(f32[256,16]{0,1:T(8,128)} %param.8) | copy-start | bytes 49156
  364.9 256.3 %copy-start.3 = (f32[256]{0:T(256)S(1)}, f32[256]{0:T(256)}, u32[]{:S(2)}) copy-start(f32[256]{0:T(256)} %param.9) | copy-start | bytes 3076
  615.9 332.5 %all-to-all-start.2 = ((bf16[16,1408,256]{2,0,1:T(8,128)(2,1)}), bf16[16,1408,256]{2,0,1:T(8,128)(2,1)}, u32[]{:S(2)}, u32[]{:S(2)}) async-start(bf16[16,1408,256]{2,0,1:T(8,128)(2,1)} %fusion), calls=%async_computation.2 | async-start | bytes 23068672 | tf_op jit(solution)/shard_map/all_to_all | solution.py:25
Sparse Core Ops, SparseCore 0:
  31.1 56.0 all-reduce.2
where the time goes:
time: 988 us; the launch traced here: 985 us
  waiting for transfers between devices  464 us (47%)
  blocking collectives  266 us (27%)
  local copies, waits for them, and re-layouts  140 us (14%)
  other arithmetic  84.8 us (9%)
  starting transfers between devices  16 us (2%)
  between operations  14.2 us (1%)
    all_gather x1, blocking collectives, per_device(): row_router = lax.all_gather(part_router, 'fsdp', axis=0, tiled=True)  257 us
    all_to_all x1, waiting for transfers between devices, per_device(): lax.all_to_all(narrow_up, 'fsdp', split_axis=2, concat_axis=1, tiled=True)  218 us
    all_to_all x1, waiting for transfers between devices, per_device(): lax.all_to_all(narrow_gate, 'fsdp', split_axis=2, concat_axis=1, tiled=True)  213 us
    unnamed x23, local copies, waits for them, and re-layouts  48.2 us
    convert_element_type x1, other arithmetic, per_device(): (train_down / jnp.expand_dims(scale_down, 2)).astype(jnp.bfloat16)  32.6 us
    pmax x1, waiting for transfers between devices, per_device(): lax.pmax((jnp.max(jnp.abs(train_gate), axis=1), jnp.max(jnp.abs(train_up)...  32.5 us
    all_to_all x2, local copies, waits for them, and re-layouts, per_device(): lax.all_to_all(narrow_down, 'fsdp', split_axis=1, concat_axis=2, tiled=True)  29.3 us
    all_to_all x2, local copies, waits for them, and re-layouts, per_device(): lax.all_to_all(narrow_gate, 'fsdp', split_axis=2, concat_axis=1, tiled=True)  29.3 us
  transfers between devices with their start and end apart: 4, of which 3 were waited for; matrix products, arithmetic and copies ran while one was open for 12% of the time, Pallas kernels for 0%

commit v1 on v0

--- a/solution.py
+++ b/solution.py
@@ -19,7 +19,12 @@
         (train_down / jnp.expand_dims(scale_down, 2)).astype(jnp.bfloat16),
     )
     ready_gate, ready_up = (
-        lax.all_to_all(narrow_gate, "fsdp", split_axis=2, concat_axis=1, tiled=True),
+        jnp.concatenate(
+            lax.all_to_all(
+                jnp.stack(jnp.split(narrow_gate, lax.axis_size("fsdp"), axis=2)), "fsdp", 0, 0
+            ),
+            axis=1,
+        ),
         lax.all_to_all(narrow_up, "fsdp", split_axis=2, concat_axis=1, tiled=True),
     )
     ready_down = lax.all_to_all(narrow_down, "fsdp", split_axis=1, concat_axis=2, tiled=True)

time: 988 us -> 972 us (0.984)
  local copies, waits for them, and re-layouts: 140 us -> 129 us
    all_to_all x2 -> x0, local copies, waits for them, and re-layouts: 29.3 us -> none  [per_device(): lax.all_to_all(narrow_gate, 'fsdp', split_axis=2, concat_axis=1, tiled=True)]
    reshape x0 -> x1, local copies, waits for them, and re-layouts: none -> 10 us  [per_device(): jnp.concatenate(lax.all_to_all(jnp.stack(jnp.split(narrow_gate, lax.axis_...]
    unnamed x23 -> x30, local copies, waits for them, and re-layouts: 48.2 us -> 56.2 us
where the time goes in v1:
time: 972 us; the launch traced here: 970 us
  waiting for transfers between devices  464 us (48%)
  blocking collectives  266 us (27%)
  local copies, waits for them, and re-layouts  129 us (13%)
  other arithmetic  80.3 us (8%)
  starting transfers between devices  16 us (2%)
  between operations  14.2 us (1%)
    all_gather x1, blocking collectives, per_device(): row_router = lax.all_gather(part_router, 'fsdp', axis=0, tiled=True)  257 us
    all_to_all x1, waiting for transfers between devices, per_device(): lax.all_to_all(narrow_up, 'fsdp', split_axis=2, concat_axis=1, tiled=True)  218 us
    all_to_all x1, waiting for transfers between devices, per_device(): lax.all_to_all(jnp.stack(jnp.split(narrow_gate, lax.axis_size('fsdp'), ax...  213 us
    unnamed x30, local copies, waits for them, and re-layouts  56.2 us
    pmax x1, waiting for transfers between devices, per_device(): lax.pmax((jnp.max(jnp.abs(train_gate), axis=1), jnp.max(jnp.abs(train_up)...  32.9 us
    convert_element_type x1, other arithmetic, per_device(): (train_down / jnp.expand_dims(scale_down, 2)).astype(jnp.bfloat16)  32.6 us
    all_to_all x2, local copies, waits for them, and re-layouts, per_device(): lax.all_to_all(narrow_down, 'fsdp', split_axis=1, concat_axis=2, tiled=True)  29.3 us
    all_to_all x2, local copies, waits for them, and re-layouts, per_device(): lax.all_to_all(narrow_up, 'fsdp', split_axis=2, concat_axis=1, tiled=True)  29.3 us
  transfers between devices with their start and end apart: 4, of which 3 were waited for; matrix products, arithmetic and copies ran while one was open for 12% of the time, Pallas kernels for 0%

profile of v1, /device:TPU:0, one launch (start us, length us, event | category | flops | bytes accessed | tf_op | source)
XLA Modules:
  0.0 970.0 jit_solution(5331135069680932767)
XLA Ops:
  7.2 10.5 %abs_reduce_fusion = f32[16,1408]{1,0:T(8,128)} fusion(f32[16,1408,256]{2,1,0:T(8,128)} %param.7), kind=kLoop, calls=%fused_computation.2 | loop fusion | flops 11511808 | bytes 23158784 | tf_op jit(solution)/shard_map/reduce_max | solution.py:12
  17.7 10.8 %abs_reduce_fusion.1 = f32[16,1408]{1,0:T(8,128)} fusion(f32[16,256,1408]{2,1,0:T(8,128)} %param.6), kind=kLoop, calls=%fused_computation.4 | loop fusion | flops 11511808 | bytes 23158784 | tf_op jit(solution)/shard_map/reduce_max | solution.py:11
  28.6 2.4 abs_reduce_fusion.2
  31.0 23.4 %copy.30 = f32[16,256,1408]{1,2,0:T(8,128)} copy(f32[16,256,1408]{2,1,0:T(8,128)} %param.5) | data formatting | bytes 46137344 | tf_op args[0]
  54.4 32.9 %all-reduce.3.cloned.1.call-done = (f32[16,1408]{1,0:T(8,128)}, f32[16,1408]{1,0:T(8,128)}, f32[16,1408]{1,0:T(8,128)}) async-done(((f32[16,1408]{1,0:T(8,128)}, f32[16,1408]{1,0:T(8,128)}, f32[16,1408]{1,0:T(8,128)}), (f32[16,1408]{1,0:T(8,128)}, f32[16,1408]{1,0:T(8,128)}, f32[16,1408]{1,0:T(8,128)})) %all-reduce.3.cloned.1.call-update) | async-done | bytes 270352 | tf_op jit(solution)/shard_map/pmax | solution.py:8
  87.2 9.8 %divide_convert_fusion.1 = bf16[16,256,1408]{1,2,0:T(8,128)(2,1)S(1)} fusion(f32[16,256,1408]{1,2,0:T(8,128)} %copy.30, f32[16,1408]{1,0:T(8,128)} %get-tuple-element.7), kind=kLoop, calls=%fused_computation.5 | loop fusion | flops 11534336 | bytes 34693120 | tf_op jit(solution)/shard_map/convert_element_type | solution.py:17
  97.1 1.2 fusion.8
  98.3 1.2 fusion.7
  99.4 1.2 fusion.6
  100.6 1.2 fusion.5
  101.8 1.2 fusion.4
  103.0 1.2 fusion.3
  104.2 1.2 fusion.2
  105.4 1.2 fusion.1
  106.6 5.4 all-to-all-start
  112.0 23.7 %copy.33 = f32[16,256,1408]{1,0,2:T(8,128)} copy(f32[16,256,1408]{2,1,0:T(8,128)} %param.6) | data formatting | bytes 46137344 | tf_op args[1]
  136.0 14.2 %divide_convert_fusion = bf16[16,256,1408]{1,0,2:T(8,128)(2,1)} fusion(f32[16,256,1408]{1,0,2:T(8,128)} %copy.33, f32[16,1408]{0,1:T(8,128)S(1)} %copy.32), kind=kLoop, calls=%fused_computation.3 | loop fusion | flops 11534336 | bytes 34693120 | tf_op jit(solution)/shard_map/convert_element_type | solution.py:18
  150.2 213.2 %all-to-all-done = bf16[8,16,256,176]{2,3,1,0:T(8,128)(2,1)} async-done(((bf16[8,16,256,176]{2,3,1,0:T(8,128)(2,1)}), bf16[8,16,256,176]{2,3,1,0:T(8,128)(2,1)}, u32[]{:S(2)}, u32[]{:S(2)}) %all-to-all-start) | async-done | bytes 11534368 | tf_op jit(solution)/shard_map/all_to_all | solution.py:23
  363.4 5.2 all-to-all-start.1
  368.9 32.6 %fusion = bf16[16,1408,256]{2,0,1:T(8,128)(2,1)} fusion(f32[16,1408,256]{2,1,0:T(8,128)} %param.7, f32[16,1408]{0,1:T(8,128)S(1)} %copy.36), kind=kLoop, calls=%fused_computation.1 | loop fusion | flops 11534336 | bytes 34693120 | tf_op jit(solution)/shard_map/convert_element_type | solution.py:19
  401.5 218.4 %all-to-all-done.1 = bf16[16,256,1408]{1,0,2:T(8,128)(2,1)} async-done(((bf16[16,256,1408]{1,0,2:T(8,128)(2,1)}), bf16[16,256,1408]{1,0,2:T(8,128)(2,1)}, u32[]{:S(2)}, u32[]{:S(2)}) %all-to-all-start.1) | async-done | bytes 11534368 | tf_op jit(solution)/shard_map/all_to_all | solution.py:28
  619.9 5.3 all-to-all-start.2
  625.3 257.3 %all_gather.6 = bf16[2048,16]{0,1:T(8,128)(2,1)S(1)} all-gather(bf16[256,16]{0,1:T(8,128)(2,1)S(1)} %multiply_convert_fusion), channel_id=1, replica_groups=mesh['ep'=4,'fsdp'=8] {'fsdp'}, dimensions={0}, use_global_device_ids=true | all-gather | bytes 73728 | tf_op jit(solution)/shard_map/all_gather | solution.py:41
  882.6 9.1 all_gather.7
  891.7 1.4 constant_dynamic-slice_fusion.2
  893.1 0.7 constant_dynamic-slice_fusion
  893.8 10.0 %copy.40 = bf16[8,16,22,8,256]{4,3,0,2,1:T(8,128)(2,1)} copy(bf16[8,16,22,8,256]{4,3,2,1,0:T(8,128)(2,1)} %bitcast.15) | data formatting | bytes 23068672 | tf_op jit(solution)/shard_map/reshape | solution.py:22
  903.8 11.3 %copy.35 = bf16[16,8,256,176]{2,1,3,0:T(8,128)(2,1)} copy(bf16[16,8,256,176]{2,0,3,1:T(8,128)(2,1)} %bitcast.11) | data formatting | bytes 23068672 | tf_op jit(solution)/shard_map/all_to_all | solution.py:28
  915.1 18.0 %all_to_all.33 = bf16[16,2048,176]{1,2,0:T(8,128)(2,1)} reshape(bf16[16,8,256,176]{2,1,3,0:T(8,128)(2,1)} %copy.35) | data formatting | bytes 23068672 | tf_op jit(solution)/shard_map/all_to_all | solution.py:28
  933.1 11.4 %copy.38 = bf16[16,176,8,256]{3,2,1,0:T(8,128)(2,1)} copy(bf16[16,176,8,256]{3,0,1,2:T(8,128)(2,1)} %bitcast.13) | data formatting | bytes 23068672 | tf_op jit(solution)/shard_map/all_to_all | solution.py:30
  944.4 18.0 %all_to_all.37 = bf16[16,176,2048]{2,1,0:T(8,128)(2,1)} reshape(bf16[16,176,8,256]{3,2,1,0:T(8,128)(2,1)} %copy.38) | data formatting | bytes 23068672 | tf_op jit(solution)/shard_map/all_to_all | solution.py:30
  962.4 0.7 copy.55
  (27 shorter events, 0.6 us)
Async XLA Ops:
  7.2 80.1 %all-reduce.3.cloned.1.call-start = ((), (), s32[]{:S(2)}) async-start(), calls=%async_computation.3 | async-start | bytes 540672 | tf_op jit(solution)/shard_map/pmax | solution.py:8
  7.2 21.3 %slice-start = ((s8[23068672]{0:T(1024)(128)(4,1)}), s8[4194304]{0:T(1024)(128)(4,1)S(1)}, s32[]{:S(2)}) async-start(s8[23068672]{0:T(1024)(128)(4,1)} %bitcast.47), calls=%async_computation.4 | async-start | bytes 8388608
  7.2 21.3 %slice-start.1 = ((s8[23068672]{0:T(1024)(128)(4,1)}), s8[4194304]{0:T(1024)(128)(4,1)S(1)}, s32[]{:S(2)}) async-start(s8[23068672]{0:T(1024)(128)(4,1)} %bitcast.47), calls=%async_computation.5 | async-start | bytes 8388608
  7.2 21.3 %slice-start.2 = ((s8[23068672]{0:T(1024)(128)(4,1)}), s8[4194304]{0:T(1024)(128)(4,1)S(1)}, s32[]{:S(2)}) async-start(s8[23068672]{0:T(1024)(128)(4,1)} %bitcast.47), calls=%async_computation.6 | async-start | bytes 8388608
  17.7 10.8 %slice-start.3 = ((s8[23068672]{0:T(1024)(128)(4,1)}), s8[4194304]{0:T(1024)(128)(4,1)S(1)}, s32[]{:S(2)}) async-start(s8[23068672]{0:T(1024)(128)(4,1)} %bitcast.47), calls=%async_computation.7 | async-start | bytes 8388608
  17.7 10.8 %slice-start.4 = ((s8[23068672]{0:T(1024)(128)(4,1)}), s8[4194304]{0:T(1024)(128)(4,1)S(1)}, s32[]{:S(2)}) async-start(s8[23068672]{0:T(1024)(128)(4,1)} %bitcast.47), calls=%async_computation.8 | async-start | bytes 8388608
  17.7 10.9 %slice-start.5 = ((s8[23068672]{0:T(1024)(128)(4,1)}), s8[2097152]{0:T(1024)(128)(4,1)S(1)}, s32[]{:S(2)}) async-start(s8[23068672]{0:T(1024)(128)(4,1)} %bitcast.47), calls=%async_computation.9 | async-start | bytes 4194304
  106.6 256.8 %all-to-all-start = ((bf16[8,16,256,176]{2,3,1,0:T(8,128)(2,1)}), bf16[8,16,256,176]{2,3,1,0:T(8,128)(2,1)}, u32[]{:S(2)}, u32[]{:S(2)}) async-start(bf16[8,16,256,176]{2,3,1,0:T(8,128)(2,1)} %fusion.1), calls=%async_computation | async-start | bytes 23068672 | tf_op jit(solution)/shard_map/all_to_all | solution.py:23
  112.0 23.7 %copy-start = (f32[16,1408]{1,0:T(8,128)S(1)}, f32[16,1408]{1,0:T(8,128)}, u32[]{:S(2)}) copy-start(f32[16,1408]{1,0:T(8,128)} %get-tuple-element.8) | copy-start | bytes 270340
  150.2 218.4 %copy-start.1 = (f32[16,1408]{1,0:T(8,128)S(1)}, f32[16,1408]{1,0:T(8,128)}, u32[]{:S(2)}) copy-start(f32[16,1408]{1,0:T(8,128)} %get-tuple-element.9) | copy-start | bytes 270340
  363.4 256.5 %all-to-all-start.1 = ((bf16[16,256,1408]{1,0,2:T(8,128)(2,1)}), bf16[16,256,1408]{1,0,2:T(8,128)(2,1)}, u32[]{:S(2)}, u32[]{:S(2)}) async-start(bf16[16,256,1408]{1,0,2:T(8,128)(2,1)} %divide_convert_fusion), calls=%async_computation.1 | async-start | bytes 23068672 | tf_op jit(solution)/shard_map/all_to_all | solution.py:28
  401.5 223.7 %copy-start.2 = (f32[256,16]{0,1:T(8,128)S(1)}, f32[256,16]{0,1:T(8,128)}, u32[]{:S(2)}) copy-start(f32[256,16]{0,1:T(8,128)} %param.8) | copy-start | bytes 49156
  401.5 223.7 %copy-start.3 = (f32[256]{0:T(256)S(1)}, f32[256]{0:T(256)}, u32[]{:S(2)}) copy-start(f32[256]{0:T(256)} %param.9) | copy-start | bytes 3076
  619.9 313.2 %all-to-all-start.2 = ((bf16[16,1408,256]{2,0,1:T(8,128)(2,1)}), bf16[16,1408,256]{2,0,1:T(8,128)(2,1)}, u32[]{:S(2)}, u32[]{:S(2)}) async-start(bf16[16,1408,256]{2,0,1:T(8,128)(2,1)} %fusion), calls=%async_computation.2 | async-start | bytes 23068672 | tf_op jit(solution)/shard_map/all_to_all | solution.py:30
Sparse Core Ops, SparseCore 0:
  31.1 56.0 all-reduce.2
